TPU v7x, 32 devices: a whole 2x2x4 slice. The times are simulated.
32 devices in a mesh: groups: 2 (over x), tm: 8 (over z, y), tile: 2 (over core).
Axes of the slice: x: 2, y: 2, z: 4, core: 2. Of those that a mesh axis runs over, the one named last changes fastest.
Arguments:
- movie: bfloat16 [4, 2304, 4096], P(('groups', 'tile'), None, 'tm'), parts along dimension 0, may hold values from 0 to 4
- cycle_weights: bfloat16 [4, 2304, 56], P(('groups', 'tile')), parts along dimension 0, may hold values from -0.75 to 0.75
- footprints: bfloat16 [4, 2304, 384], P(('groups', 'tile')), parts along dimension 0, may hold values from 0.19921875 to 1
- traces: bfloat16 [4, 384, 4096], P(('groups', 'tile'), None, 'tm'), parts along dimension 0, may hold values from 0 to 1.5
- centre_row: int32 [4, 384], P(('groups', 'tile')), parts along dimension 0, may hold values from 0 to 47
- centre_col: int32 [4, 384], P(('groups', 'tile')), parts along dimension 0, may hold values from 0 to 47
- radius: int32 [4, 384], P(('groups', 'tile')), parts along dimension 0, may hold values from 4 to 9
- comp_count: int32 [4], P(('groups', 'tile')), parts along dimension 0, may hold values from 64 to 384
Outputs:
- new_footprints: bfloat16 [4, 2304, 384], P(('groups', 'tile')), parts along dimension 0
- new_traces: bfloat16 [4, 384, 4096], P(('groups', 'tile'), None, 'tm'), parts along dimension 0
There are 2 independent parts, one for each index of `groups`. A program takes and returns all parts, laid end to end along the dimension named above; each array names one. Nothing has to cross between parts.
All inputs are finite; a program needn't handle non-finite values.
Results may differ from a plain program's by a relative error of at most 0.0034.
Values may be sent and summed in bfloat16 or wider, within the bound.
A program may use at most 64 MiB of HBM per device.

v0:
```python
import jax
import jax.numpy as jnp
from jax import lax
from jax.sharding import PartitionSpec as P

TILE_SIDE = 48
CYCLE = 8
KMAX = 384
PASSES = 2


RIDGE_TERM = 1.0


def with_halo(block, sides, width):
    for axis, dim in sides:
        count = lax.axis_size(axis)
        forward = [(i, i + 1) for i in range(count - 1)]
        backward = [(target, source) for source, target in forward]
        low = lax.ppermute(
            lax.slice_in_dim(block, block.shape[dim] - width, None, axis=dim), axis, forward
        )
        high = lax.ppermute(lax.slice_in_dim(block, 0, width, axis=dim), axis, backward)
        block = jnp.concatenate([low, block, high], axis=dim)
    return block


def cycle_offsets():
    found = []
    for row_step in range(-CYCLE, CYCLE + 1):
        for col_step in range(-CYCLE, CYCLE + 1):
            dist_sq = row_step * row_step + col_step * col_step
            if CYCLE * CYCLE <= dist_sq < (CYCLE + 1) * (CYCLE + 1):
                found.append((row_step, col_step))
    return found


def cycle_back(weights, window):
    frames = window.shape[2]
    grid_w = weights.reshape(TILE_SIDE, TILE_SIDE, -1)
    total = jnp.zeros((TILE_SIDE, TILE_SIDE, frames), jnp.float32)
    for index, (row_step, col_step) in enumerate(cycle_offsets()):
        top = CYCLE + row_step
        left = CYCLE + col_step
        piece = window[top : top + TILE_SIDE, left : left + TILE_SIDE, :].astype(jnp.float32)
        total = total + grid_w[:, :, index : index + 1].astype(jnp.float32) * piece
    return total.reshape(TILE_SIDE * TILE_SIDE, frames).astype(jnp.bfloat16)


def keep_mask(row_at, col_at, reach, count):
    pixel = jnp.arange(TILE_SIDE * TILE_SIDE, dtype=jnp.int32)
    row_gap = (pixel // TILE_SIDE)[:, None] - row_at[None, :]
    col_gap = (pixel % TILE_SIDE)[:, None] - col_at[None, :]
    inside = row_gap * row_gap + col_gap * col_gap <= (reach * reach)[None, :]
    live = jnp.arange(KMAX, dtype=jnp.int32) < count
    return (inside & live[None, :], live)


def footprint_move(foot, keep, grad_a, den_c):
    moved = jnp.maximum(foot.astype(jnp.float32) - grad_a / den_c[None, :], 0.0)
    return jnp.where(keep, moved, 0.0).astype(jnp.bfloat16)


def shards(movie, cycle_weights, footprints, traces, centre_row, centre_col, radius, comp_count):
    zero = jnp.zeros((), jnp.bfloat16)
    keep, live = keep_mask(centre_row[0], centre_col[0], radius[0], comp_count[0])
    foot = jnp.where(keep, footprints[0], zero)
    trace = jnp.where(live[:, None], traces[0], zero)
    den_a = jnp.sum(jnp.square(foot.astype(jnp.float32)), axis=0) + RIDGE_TERM
    frames_here = movie.shape[2]
    movie_f = movie[0].astype(jnp.float32)
    back = None
    for sweep in range(PASSES):
        prod = jnp.dot(foot, trace, preferred_element_type=jnp.float32)
        resid = (movie_f - prod).astype(jnp.bfloat16).reshape(TILE_SIDE, TILE_SIDE, frames_here)
        widened = with_halo(resid, (("tile", 1),), CYCLE)
        window = jnp.pad(widened, ((CYCLE, CYCLE), (0, 0), (0, 0)))
        back = cycle_back(cycle_weights[0], window)
        err = (prod + back.astype(jnp.float32) - movie_f).astype(jnp.bfloat16)
        grad = lax.dot_general(
            foot, err, (((0,), (0,)), ((), ())), preferred_element_type=jnp.float32
        )
        moved = jnp.maximum(trace.astype(jnp.float32) - grad / den_a[:, None], 0.0)
        trace = jnp.where(live[:, None], moved, 0.0).astype(jnp.bfloat16)
    prod = jnp.dot(foot, trace, preferred_element_type=jnp.float32)
    ferr = (prod + back.astype(jnp.float32) - movie_f).astype(jnp.bfloat16)
    energy = jnp.sum(jnp.square(trace.astype(jnp.float32)), axis=1)
    share_rows = foot.shape[0] // lax.axis_size("tm")
    grad_share = lax.psum_scatter(
        lax.dot_general(ferr, trace, (((1,), (1,)), ((), ())), preferred_element_type=jnp.float32),
        "tm",
        scatter_dimension=0,
        tiled=True,
    )
    energy_all = lax.psum(energy, "tm")
    first_row = lax.axis_index("tm") * share_rows
    foot_share = lax.dynamic_slice_in_dim(foot, first_row, share_rows, 0)
    keep_share = lax.dynamic_slice_in_dim(keep, first_row, share_rows, 0)
    moved_share = footprint_move(foot_share, keep_share, grad_share, energy_all + RIDGE_TERM)
    new_foot = lax.all_gather(moved_share, "tm", axis=0, tiled=True)
    return (new_foot[None], trace[None])


def solution(mesh):
    in_specs = (
        P(("groups", "tile"), None, "tm"),
        P(("groups", "tile"), None, None),
        P(("groups", "tile"), None, None),
        P(("groups", "tile"), None, "tm"),
        P(("groups", "tile"), None),
        P(("groups", "tile"), None),
        P(("groups", "tile"), None),
        P(("groups", "tile")),
    )
    out_specs = (P(("groups", "tile"), None, None), P(("groups", "tile"), None, "tm"))
    return jax.shard_map(shards, mesh=mesh, in_specs=in_specs, out_specs=out_specs, check_vma=False)
```

profile of v0, /device:TPU:0, one launch (start us, length us, event | category | flops | bytes accessed | tf_op | source)
XLA Modules:
  0.0 274.7 jit_solution(6336495007161943169)
XLA Ops:
  7.2 0.0 reduce-scatter.2.cloned.1.call-start
  7.9 0.7 multiply_reduce_fusion.2
  8.6 0.7 reduce
  9.3 0.7 reduce.1
  10.0 0.0 copy-start.5
  10.0 5.4 %fusion.1 = (bf16[2304,512]{1,0:T(8,128)(2,1)S(1)}, f32[2304,512]{1,0:T(8,128)}) fusion(bf16[1,2304,512]{2,1,0:T(8,128)(2,1)} %param.8, bf16[1,384,512]{2,1,0:T(8,128)(2,1)} %param.11, pred[384]{0:T(512)(128)(4,1)S(1)} %iota_compare_fusion.2, bf16[1,2304,384]{2,1,0:T(8,128)(2,1)} %param.10, s32[384]{0:T(512)S(1)} %multiply_reduce_fusion.2, ...), kind=kOutput, calls=%fused_computation.10 | convolution fusion | flops 916783104 | bytes 11623296 | tf_op jit(solution)/shard_map/dot_general | solution.py:74
  15.4 0.0 copy-start
  15.4 1.4 copy-done
  16.9 0.9 fusion.121
  17.8 2.4 collective-permute-start
  20.2 1.3 collective-permute-start.1
  21.5 0.0 copy-done.5
  21.5 0.9 reshape_squeeze.4
  22.5 0.0 copy-start.1
  22.6 3.7 %multiply_reduce_fusion = (f32[384]{0:T(512)S(1)}, bf16[2304,384]{1,0:T(8,128)(2,1)S(1)}) fusion(bf16[1,2304,384]{2,1,0:T(8,128)(2,1)} %param.10, pred[384]{0:T(512)(128)(4,1)S(1)} %iota_compare_fusion.2, s32[384]{0:T(512)S(1)} %multiply_reduce_fusion.2, s32[384]{0:T(512)S(1)} %reduce.1, s32[2304]{0:T(1024)S(1)} %get-tuple-element.70, s32[384]{0:T(512)S(1)} %reduce, ...), kind=kLoop, calls=%fused_computation.23 | loop fusion | flops 9731712 | bytes 3563904 | tf_op jit(solution)/shard_map/reduce_sum | solution.py:69
  26.3 0.0 collective-permute-done
  26.3 0.0 collective-permute-done.1
  26.3 0.0 copy-done.1
  26.3 0.0 slice-start
  26.3 0.6 select_maximum_fusion.2
  26.9 0.0 copy-start.2
  26.9 0.0 copy-start.6
  26.9 0.0 slice-start.1
  26.9 43.9 %add_convert_fusion.1 = bf16[48,48,512]{2,1,0:T(8,128)(2,1)S(1)} fusion(bf16[64,64,512]{2,1,0:T(8,128)(2,1)S(1)} %select_maximum_fusion.2, bf16[48,8,512]{2,1,0:T(8,128)(2,1)S(1)} %collective-permute-done.1, bf16[48,48,512]{2,1,0:T(8,128)(2,1)S(1)} %bitcast.347, bf16[48,8,512]{2,1,0:T(8,128)(2,1)S(1)} %collective-permute-done, ...), kind=kLoop, calls=%fused_computation.16 | loop fusion | flops 205258752 | bytes 133423104 | tf_op jit(solution)/shard_map/convert_element_type | solution.py:47
  70.8 0.0 slice-done
  70.9 0.0 copy-done.2
  70.9 0.0 copy-done.6
  70.9 0.0 slice-done.1
  70.9 1.4 fusion.38
  72.3 1.4 fusion.3
  73.7 0.1 fusion.120
  73.7 3.1 %collective-permute-start.2 = (bf16[48,8,512]{2,1,0:T(8,128)(2,1)S(1)}, bf16[48,8,512]{2,1,0:T(8,128)(2,1)S(1)}, u32[]{:S(2)}, u32[]{:S(2)}) collective-permute-start(bf16[48,8,512]{2,1,0:T(8,128)(2,1)S(1)} %get-tuple-element.4), channel_id=1, source_target_pairs={{0,1},{2,3},{4,5},{6,7},{8,9},{10,11},{12,13},{14,15},{16,17},{18,... | collective-permute-start | bytes 1179656 | tf_op jit(solution)/shard_map/ppermute | solution.py:20
  76.8 1.5 collective-permute-start.3
  78.3 0.0 collective-permute-done.2
  78.3 2.1 collective-permute-done.3
  80.4 0.6 select_maximum_fusion
  81.0 43.9 %add_convert_fusion = bf16[48,48,512]{2,1,0:T(8,128)(2,1)S(1)} fusion(bf16[64,64,512]{2,1,0:T(8,128)(2,1)S(1)} %select_maximum_fusion, bf16[48,8,512]{2,1,0:T(8,128)(2,1)S(1)} %collective-permute-done.3, bf16[48,48,512]{2,1,0:T(8,128)(2,1)S(1)} %bitcast.344, bf16[48,8,512]{2,1,0:T(8,128)(2,1)S(1)} %collective-permute-done.2, ...), kind=kLoop, calls=%fused_computation.15 | loop fusion | flops 205258752 | bytes 133423104 | tf_op jit(solution)/shard_map/convert_element_type | solution.py:47
  124.9 0.0 copy-start.3
  124.9 1.4 copy-done.3
  126.3 1.3 fusion.41
  127.6 0.0 copy-start.4
  127.6 7.2 %fusion.25 = f32[2304,384]{1,0:T(8,128)} fusion(bf16[2304,512]{1,0:T(8,128)(2,1)} %bitcast.349, bf16[2304,384]{1,0:T(8,128)(2,1)S(1)} %get-tuple-element.3, bf16[1,2304,512]{2,1,0:T(8,128)(2,1)} %param.8, f32[384,512]{1,0:T(8,128)S(1)} %fusion.41, bf16[384,512]{1,0:T(8,128)(2,1)S(1)} %fusion.38, pred[384]{0:T(512)(128)(4,1)S(1)} %iota_compare_fusion.2), kind=kOutput, calls=%fused_computation.46 | convolution fusion | flops 1819803648 | bytes 11207040 | tf_op jit(solution)/shard_map/dot_general | solution.py:90
  134.8 0.0 copy-done.4
  134.8 0.0 reduce-scatter.2.cloned.1.call-update
  134.8 0.0 all-gather.2.cloned.1.call-start
  134.9 1.5 fusion.7
  136.4 2.1 fusion.45
  138.5 23.1 %psum.7 = f32[384]{0:T(512)S(1)} all-reduce(f32[384]{0:T(512)S(1)} %get-tuple-element.9), channel_id=1, replica_groups=mesh['groups'=2,'tm'=8,'tile'=2] {'tm'}, use_global_device_ids=true, to_apply=%region_3.4 | all-reduce | flops 384 | bytes 3072 | tf_op jit(solution)/shard_map/psum | solution.py:95
  161.6 55.1 %reduce-scatter.2.cloned.1.call-done = f32[288,384]{1,0:T(8,128)} async-done(((f32[2304,384]{1,0:T(8,128)}), f32[288,384]{1,0:T(8,128)}) %reduce-scatter.2.cloned.1.call-update) | async-done | bytes 442384 | tf_op jit(solution)/shard_map/reduce_scatter | solution.py:89
  216.7 1.8 select_convert_fusion.3
  218.5 0.0 all-gather.2.cloned.1.call-update
  218.5 46.4 %all-gather.2.cloned.1.call-done = bf16[2304,384]{1,0:T(8,128)(2,1)} async-done(((bf16[288,384]{1,0:T(8,128)(2,1)}), bf16[2304,384]{1,0:T(8,128)(2,1)}) %all-gather.2.cloned.1.call-update) | async-done | bytes 1769488 | tf_op jit(solution)/shard_map/all_gather | solution.py:100
  265.0 2.9 %copy.12 = bf16[1,2304,384]{2,1,0:T(8,128)(2,1)} copy(bf16[1,2304,384]{2,1,0:T(8,128)(2,1)} %bitcast.351) | data formatting | bytes 3538944
  (8 shorter events, 0.1 us)
Async XLA Ops:
  7.2 209.5 %reduce-scatter.2.cloned.1.call-start = ((), (), s32[]{:S(2)}) async-start(), calls=%async_computation.1 | async-start | bytes 3981312 | tf_op jit(solution)/shard_map/reduce_scatter | solution.py:89
  10.0 11.5 %copy-start.5 = (bf16[1,2304,56]{1,2,0:T(8,128)(2,1)S(1)}, bf16[1,2304,56]{1,2,0:T(8,128)(2,1)}, u32[]{:S(2)}) copy-start(bf16[1,2304,56]{1,2,0:T(8,128)(2,1)} %param.9) | copy-start | bytes 774148
  15.4 1.4 copy-start
  17.8 8.5 %collective-permute-start = (bf16[48,8,512]{2,1,0:T(8,128)(2,1)}, bf16[48,8,512]{2,1,0:T(8,128)(2,1)S(1)}, u32[]{:S(2)}, u32[]{:S(2)}) collective-permute-start(bf16[48,8,512]{2,1,0:T(8,128)(2,1)} %get-tuple-element.6), channel_id=1, source_target_pairs={{0,1},{2,3},{4,5},{6,7},{8,9},{10,11},{12,13},{14,15},{16,17},{18,... | collective-permute-start | bytes 1179656 | tf_op jit(solution)/shard_map/ppermute | solution.py:20
  20.2 6.1 %collective-permute-start.1 = (bf16[48,8,512]{2,1,0:T(8,128)(2,1)}, bf16[48,8,512]{2,1,0:T(8,128)(2,1)S(1)}, u32[]{:S(2)}, u32[]{:S(2)}) collective-permute-start(bf16[48,8,512]{2,1,0:T(8,128)(2,1)} %get-tuple-element.7), channel_id=1, source_target_pairs={{1,0},{3,2},{5,4},{7,6},{9,8},{11,10},{13,12},{15,14},{17,16},{19,... | collective-permute-start | bytes 1179656 | tf_op jit(solution)/shard_map/ppermute | solution.py:23
  22.5 3.9 %copy-start.1 = (bf16[2304,512]{1,0:T(8,128)(2,1)S(1)}, bf16[2304,512]{1,0:T(8,128)(2,1)}, u32[]{:S(2)}) copy-start(bf16[2304,512]{1,0:T(8,128)(2,1)} %copy-done) | copy-start | bytes 7077892
  26.3 44.5 %slice-start = ((s8[4718592]{0:T(1024)(128)(4,1)}), s8[4194304]{0:T(1024)(128)(4,1)S(1)}, s32[]{:S(2)}) async-start(s8[4718592]{0:T(1024)(128)(4,1)} %bitcast.352), calls=%async_computation.3 | async-start | bytes 8388608
  26.9 43.9 %copy-start.2 = (bf16[1,2304,512]{2,1,0:T(8,128)(2,1)S(1)}, bf16[1,2304,512]{2,1,0:T(8,128)(2,1)}, u32[]{:S(2)}) copy-start(bf16[1,2304,512]{2,1,0:T(8,128)(2,1)} %param.8) | copy-start | bytes 7077892
  26.9 43.9 %copy-start.6 = (bf16[1,384,512]{2,1,0:T(8,128)(2,1)S(1)}, bf16[1,384,512]{2,1,0:T(8,128)(2,1)}, u32[]{:S(2)}) copy-start(bf16[1,384,512]{2,1,0:T(8,128)(2,1)} %param.11) | copy-start | bytes 1179652
  26.9 43.9 %slice-start.1 = ((s8[4718592]{0:T(1024)(128)(4,1)}), s8[524288]{0:T(1024)(128)(4,1)S(1)}, s32[]{:S(2)}) async-start(s8[4718592]{0:T(1024)(128)(4,1)} %bitcast.352), calls=%async_computation.4 | async-start | bytes 1048576
  73.7 4.6 %collective-permute-start.2 = (bf16[48,8,512]{2,1,0:T(8,128)(2,1)S(1)}, bf16[48,8,512]{2,1,0:T(8,128)(2,1)S(1)}, u32[]{:S(2)}, u32[]{:S(2)}) collective-permute-start(bf16[48,8,512]{2,1,0:T(8,128)(2,1)S(1)} %get-tuple-element.4), channel_id=1, source_target_pairs={{0,1},{2,3},{4,5},{6,7},{8,9},{10,11},{12,13},{14,15},{16,17},{18,... | collective-permute-start | bytes 1179656 | tf_op jit(solution)/shard_map/ppermute | solution.py:20
  76.8 3.6 %collective-permute-start.3 = (bf16[48,8,512]{2,1,0:T(8,128)(2,1)S(1)}, bf16[48,8,512]{2,1,0:T(8,128)(2,1)S(1)}, u32[]{:S(2)}, u32[]{:S(2)}) collective-permute-start(bf16[48,8,512]{2,1,0:T(8,128)(2,1)S(1)} %get-tuple-element.5), channel_id=1, source_target_pairs={{1,0},{3,2},{5,4},{7,6},{9,8},{11,10},{13,12},{15,14},{17,16},{19,... | collective-permute-start | bytes 1179656 | tf_op jit(solution)/shard_map/ppermute | solution.py:23
  124.9 1.4 copy-start.3
  127.6 7.2 %copy-start.4 = (f32[384,512]{1,0:T(8,128)}, f32[384,512]{1,0:T(8,128)S(1)}, u32[]{:S(2)}) copy-start(f32[384,512]{1,0:T(8,128)S(1)} %fusion.41) | copy-start | bytes 2359300
  134.8 130.2 %all-gather.2.cloned.1.call-start = ((), (), s32[]{:S(2)}) async-start(), calls=%async_computation.2 | async-start | bytes 1990656 | tf_op jit(solution)/shard_map/all_gather | solution.py:100
Sparse Core Ops, SparseCore 0:
  134.9 81.7 reduce-scatter.1
  219.5 45.4 all-gather.1
where the time goes:
time: 275 us
  waiting for transfers between devices  104 us (38%)
  other arithmetic  100 us (36%)
  blocking collectives  23.1 us (8%)
  matrix products  16.7 us (6%)
  between operations  15 us (5%)
  starting transfers between devices  8.32 us (3%)
  local copies, waits for them, and re-layouts  7.67 us (3%)
    convert_element_type x2, other arithmetic, cycle_back(): return total.reshape(TILE_SIDE * TILE_SIDE, frames).astype(jnp.bfloat16)  87.8 us
    reduce_scatter x1, waiting for transfers between devices, shards(): lax.psum_scatter(lax.dot_general(ferr, trace, (((1,), (1,)), ((), ())), p...  55.1 us
    all_gather x1, waiting for transfers between devices, shards(): new_foot = lax.all_gather(moved_share, 'tm', axis=0, tiled=True)  46.4 us
    psum x1, blocking collectives, shards(): energy_all = lax.psum(energy, 'tm')  23.1 us
    dot_general x1, matrix products, shards(): lax.dot_general(ferr, trace, (((1,), (1,)), ((), ())), preferred_element_...  7.19 us
    dot_general x2, matrix products, shards(): prod = jnp.dot(foot, trace, preferred_element_type=jnp.float32)  6.83 us
    unnamed x19, local copies, waits for them, and re-layouts  5.74 us
  transfers between devices with their start and end apart: 6, of which 3 were waited for; matrix products, arithmetic and copies ran while one was open for 3% of the time, Pallas kernels for 0%

commit v1 on v0

v1 whole, which is shorter than its diff:
```python
import functools

import jax
import jax.numpy as jnp
import numpy as np
from jax import lax
from jax.experimental import pallas as pl
from jax.experimental.pallas import tpu as pltpu
from jax.sharding import PartitionSpec as P

SIDE = 48
CYCLE = 8
WIDE = SIDE + 2 * CYCLE
FOLD = 24
PASSES = 2
RIDGE_TERM = 1.0
BLOCK = 4
SPAN = BLOCK + 2 * CYCLE
LANES = 128
F32 = jnp.float32
BF16 = jnp.bfloat16
MESH = pl.DeviceIdType.MESH


def cycle_offsets():
    found = []
    for row_step in range(-CYCLE, CYCLE + 1):
        for col_step in range(-CYCLE, CYCLE + 1):
            dist_sq = row_step * row_step + col_step * col_step
            if CYCLE * CYCLE <= dist_sq < (CYCLE + 1) * (CYCLE + 1):
                found.append((row_step, col_step))
    return found


def spread_tables():
    offsets = cycle_offsets()
    width = WIDE * (2 * CYCLE + 2)
    tables = np.zeros((2, len(offsets), width), np.float32)
    for index, (row_step, col_step) in enumerate(offsets):
        for odd in range(2):
            tables[odd, index, (row_step + CYCLE + odd) * WIDE + col_step + CYCLE] = 1.0
    return tables


def fold_columns(rows):
    return rows[:, :FOLD] + rows[:, FOLD:]


def kernel(
    n, s, shares,
    movie, weights, prints, traces, row_at, col_at, reach, count, tables,
    new_foot, new_trace,
    foot, band, pm, win, errs, backs, trace, gacc, inv_den, col_sq,
    halo_out, halo_in, part, own, arrived, energy_out, energy_in, gathered,
    halo_sems, part_sems, energy_sems, gather_sems,
):
    me = lax.axis_index("tm")
    tile = lax.axis_index("tile")
    frames = movie.shape[2]
    comps = prints.shape[2]
    blocks = SIDE // BLOCK

    barrier = pltpu.get_barrier_semaphore()
    pl.semaphore_signal(barrier, inc=1, device_id={"tile": 1 - tile}, device_id_type=MESH)

    def greet(t, carry):
        peer = lax.rem(me + 1 + t, n)
        pl.semaphore_signal(barrier, inc=1, device_id={"tm": peer}, device_id_type=MESH)
        return carry

    lax.fori_loop(0, n - 1, greet, 0)

    live_row = lax.broadcasted_iota(jnp.int32, (1, comps), 1) < count[0]
    bound = jnp.where(live_row, reach[...] * reach[...], -1)
    col_gap = lax.broadcasted_iota(jnp.int32, (SIDE, comps), 0) - col_at[...]
    col_sq[...] = col_gap * col_gap

    def mask_row(r, total):
        row_gap = r - row_at[...]
        keep = col_sq[...] <= bound - row_gap * row_gap
        kept = jnp.where(keep, prints[r].astype(F32), 0.0)
        foot[r] = kept.astype(BF16)
        return total + kept * kept

    total = lax.fori_loop(0, SIDE, mask_row, jnp.zeros((SIDE, comps), F32))
    den = jnp.sum(total, axis=0, keepdims=True) + RIDGE_TERM
    inv_den[...] = jnp.transpose(jnp.broadcast_to(1.0 / den, (LANES, comps)))
    live = lax.broadcasted_iota(jnp.int32, (comps, LANES), 0) < count[0]
    for q in range(frames // LANES):
        cols = slice(q * LANES, (q + 1) * LANES)
        trace[:, cols] = jnp.where(live, traces[:, cols].astype(F32), 0.0).astype(BF16)
    win[0:CYCLE] = jnp.zeros((CYCLE, WIDE, frames), BF16)
    win[CYCLE + SIDE : WIDE] = jnp.zeros((CYCLE, WIDE, frames), BF16)
    pl.semaphore_wait(barrier, n)

    def halo_copy(sweep):
        return pltpu.make_async_remote_copy(
            src_ref=halo_out.at[sweep],
            dst_ref=halo_in.at[sweep],
            send_sem=halo_sems.at[0, sweep],
            recv_sem=halo_sems.at[1, sweep],
            device_id={"tile": 1 - tile},
            device_id_type=MESH,
        )

    def build_band(b, carry):
        for i in range(BLOCK):
            spread = jnp.dot(weights[b * BLOCK + i], tables[i % 2], preferred_element_type=F32)
            first = (i // 2) * LANES
            rows = slice(i * SIDE, (i + 1) * SIDE)
            if first > 0:
                band[b, rows, 0:first] = jnp.zeros((SIDE, first), BF16)
            for q in range(spread.shape[1] // LANES):
                skewed = pltpu.roll(
                    spread[:, q * LANES : (q + 1) * LANES], 0, 1, stride=1, stride_axis=0
                )
                band[b, rows, first + q * LANES : first + (q + 1) * LANES] = skewed.astype(BF16)
            last = first + spread.shape[1]
            if last < SPAN * WIDE:
                band[b, rows, last:] = jnp.zeros((SIDE, SPAN * WIDE - last), BF16)
        return carry

    for sweep in range(PASSES):

        def residual(b, carry):
            rows = pl.ds(b * BLOCK, BLOCK)
            prod = jnp.dot(
                foot[rows].reshape(BLOCK * SIDE, comps), trace[...], preferred_element_type=F32
            )
            diff = prod.reshape(BLOCK, SIDE, frames) - movie[rows].astype(F32)
            pm[rows] = diff
            edge = jnp.where(tile == 0, -diff[:, SIDE - CYCLE :], -diff[:, :CYCLE])
            halo_out[sweep, b] = edge.reshape(BLOCK * CYCLE, frames).astype(BF16)
            return carry

        lax.fori_loop(0, blocks, residual, 0)
        copy = halo_copy(sweep)
        copy.start()
        if sweep == 0:
            lax.fori_loop(0, blocks, build_band, 0)
        copy.wait_recv()

        def fill(b, carry):
            rows = pl.ds(b * BLOCK, BLOCK)
            edge = halo_in[sweep, b].astype(F32).reshape(BLOCK, CYCLE, frames)
            low = jnp.where(tile == 0, 0.0, edge)
            high = jnp.where(tile == 0, edge, 0.0)
            whole = jnp.concatenate([low, -pm[rows], high], axis=1)
            win[pl.ds(CYCLE + b * BLOCK, BLOCK)] = whole.astype(BF16)
            return carry

        lax.fori_loop(0, blocks, fill, 0)

        def background(b, carry):
            rows = pl.ds(b * BLOCK, BLOCK)
            seen = win[pl.ds(b * BLOCK, SPAN)].reshape(SPAN * WIDE, frames)
            back = jnp.dot(band[b], seen, preferred_element_type=F32).astype(BF16)
            back = back.reshape(BLOCK, SIDE, frames)
            if sweep == PASSES - 1:
                backs[rows] = back
            errs[rows] = (pm[rows] + back.astype(F32)).astype(BF16)
            return carry

        lax.fori_loop(0, blocks, background, 0)

        depth = 16
        gacc[...] = jnp.zeros_like(gacc)

        def descend(j, carry):
            rows = pl.ds(j * depth, depth)
            gacc[...] += lax.dot_general(
                foot[rows].reshape(depth * SIDE, comps),
                errs[rows].reshape(depth * SIDE, frames),
                (((0,), (0,)), ((), ())),
                preferred_element_type=F32,
            )
            return carry

        lax.fori_loop(0, SIDE // depth, descend, 0)
        for q in range(frames // LANES):
            cols = slice(q * LANES, (q + 1) * LANES)
            moved = jnp.maximum(trace[:, cols].astype(F32) - gacc[:, cols] * inv_den[...], 0.0)
            trace[:, cols] = jnp.where(live, moved, 0.0).astype(BF16)

    new_trace[...] = trace[...]
    squares = jnp.zeros((comps, LANES), F32)
    for q in range(frames // LANES):
        now = trace[:, q * LANES : (q + 1) * LANES].astype(F32)
        squares = squares + now * now
    energy = jnp.sum(jnp.transpose(squares), axis=0, keepdims=True)
    energy_out[...] = jnp.broadcast_to(energy, energy_out.shape)

    def energy_copy(peer, sender):
        return pltpu.make_async_remote_copy(
            src_ref=energy_out,
            dst_ref=energy_in.at[sender],
            send_sem=energy_sems.at[0, peer],
            recv_sem=energy_sems.at[1, sender],
            device_id={"tm": peer},
            device_id_type=MESH,
        )

    def part_copy(peer, sender):
        return pltpu.make_async_remote_copy(
            src_ref=part.at[peer],
            dst_ref=arrived.at[sender],
            send_sem=part_sems.at[0, peer],
            recv_sem=part_sems.at[1, sender],
            device_id={"tm": peer},
            device_id_type=MESH,
        )

    def gather_copy(peer, sender):
        return pltpu.make_async_remote_copy(
            src_ref=gathered.at[sender],
            dst_ref=gathered.at[sender],
            send_sem=gather_sems.at[0, peer],
            recv_sem=gather_sems.at[1, sender],
            device_id={"tm": peer},
            device_id_type=MESH,
        )

    def owns(index, do):
        if shares == n:
            do()
        else:
            pl.when(index < shares)(do)

    def over_peers(do):
        def step(t, carry):
            do(lax.rem(me + 1 + t, n))
            return carry

        lax.fori_loop(0, n - 1, step, 0)

    over_peers(lambda peer: owns(peer, lambda: energy_copy(peer, me).start()))

    def share_of(share):
        top, low = pl.ds(share * s, s), pl.ds(FOLD + share * s, s)
        feet = jnp.concatenate([foot[top], foot[low]], axis=0).reshape(2 * s * SIDE, comps)
        prod = jnp.dot(feet, trace[...], preferred_element_type=F32)
        back = jnp.concatenate([backs[top], backs[low]], axis=0).reshape(2 * s * SIDE, frames)
        seen = jnp.concatenate([movie[top], movie[low]], axis=0).reshape(2 * s * SIDE, frames)
        ferr = (prod + back.astype(F32) - seen.astype(F32)).astype(BF16)
        grad = lax.dot_general(
            ferr, trace[...], (((1,), (1,)), ((), ())), preferred_element_type=F32
        )
        grad = jnp.where(feet.astype(F32) > 0.0, grad, 0.0).reshape(2 * s, SIDE, comps)
        return fold_columns(grad[:s] + grad[s:]).reshape(s * FOLD, comps)

    def send_share(share):
        part[share] = share_of(share).astype(BF16)
        part_copy(share, me).start()

    over_peers(lambda peer: owns(peer, lambda: send_share(peer)))

    def settle():
        own[...] = share_of(me)
        energy_in[me] = energy_out[...]

        def take(peer):
            energy_copy(me, peer).wait_recv()
            part_copy(me, peer).wait_recv()
            own[...] += arrived[peer].astype(F32)
            energy_in[me] += energy_in[peer]

        over_peers(take)
        den_c = energy_in[me][:1] + RIDGE_TERM
        top, low = pl.ds(me * s, s), pl.ds(FOLD + me * s, s)
        feet = fold_columns(foot[top].astype(F32) + foot[low].astype(F32)).reshape(s * FOLD, comps)
        gathered[me] = jnp.maximum(feet - own[...] / den_c, 0.0).astype(BF16)
        over_peers(lambda peer: gather_copy(peer, me).start())

    owns(me, settle)

    def unfold(share):
        values = gathered[share].astype(F32).reshape(s, FOLD, comps)
        values = jnp.concatenate([values, values], axis=1)
        for half in range(2):
            rows = pl.ds(half * FOLD + share * s, s)
            new_foot[rows] = jnp.where(foot[rows].astype(F32) > 0.0, values, 0.0).astype(BF16)

    owns(me, lambda: unfold(me))

    def receive(peer):
        gather_copy(me, peer).wait_recv()
        unfold(peer)

    over_peers(lambda peer: owns(peer, lambda: receive(peer)))

    for sweep in range(PASSES):
        halo_copy(sweep).wait_send()

    def drain(peer):
        owns(peer, lambda: energy_copy(peer, me).wait_send())
        owns(peer, lambda: part_copy(peer, me).wait_send())
        owns(me, lambda: gather_copy(peer, me).wait_send())

    over_peers(drain)


def shards(movie, cycle_weights, footprints, traces, centre_row, centre_col, radius, comp_count):
    n = lax.axis_size("tm")
    frames = movie.shape[2]
    comps = footprints.shape[2]
    s = -(-FOLD // n)
    while FOLD % s:
        s += 1
    shares = FOLD // s
    blocks = SIDE // BLOCK
    tables = jnp.asarray(spread_tables(), BF16)
    vmem = pl.BlockSpec(memory_space=pltpu.VMEM)
    smem = pl.BlockSpec(memory_space=pltpu.SMEM)
    new_foot, new_trace = pl.pallas_call(
        functools.partial(kernel, n, s, shares),
        out_shape=(
            jax.ShapeDtypeStruct((SIDE, SIDE, comps), BF16),
            jax.ShapeDtypeStruct((comps, frames), BF16),
        ),
        in_specs=[vmem] * 7 + [smem, vmem],
        out_specs=(vmem, vmem),
        scratch_shapes=[
            pltpu.VMEM((SIDE, SIDE, comps), BF16),
            pltpu.VMEM((blocks, BLOCK * SIDE, SPAN * WIDE), BF16),
            pltpu.VMEM((SIDE, SIDE, frames), F32),
            pltpu.VMEM((WIDE, WIDE, frames), BF16),
            pltpu.VMEM((SIDE, SIDE, frames), BF16),
            pltpu.VMEM((SIDE, SIDE, frames), BF16),
            pltpu.VMEM((comps, frames), BF16),
            pltpu.VMEM((comps, frames), F32),
            pltpu.VMEM((comps, LANES), F32),
            pltpu.VMEM((SIDE, comps), jnp.int32),
            pltpu.VMEM((PASSES, blocks, BLOCK * CYCLE, frames), BF16),
            pltpu.VMEM((PASSES, blocks, BLOCK * CYCLE, frames), BF16),
            pltpu.VMEM((n, s * FOLD, comps), BF16),
            pltpu.VMEM((s * FOLD, comps), F32),
            pltpu.VMEM((n, s * FOLD, comps), BF16),
            pltpu.VMEM((8, comps), F32),
            pltpu.VMEM((n, 8, comps), F32),
            pltpu.VMEM((n, s * FOLD, comps), BF16),
            pltpu.SemaphoreType.DMA((2, PASSES)),
            pltpu.SemaphoreType.DMA((2, n)),
            pltpu.SemaphoreType.DMA((2, n)),
            pltpu.SemaphoreType.DMA((2, n)),
        ],
        compiler_params=pltpu.CompilerParams(
            collective_id=0, has_side_effects=True, vmem_limit_bytes=60 * 1024 * 1024
        ),
    )(
        movie.reshape(SIDE, SIDE, frames),
        cycle_weights.reshape(SIDE, SIDE, -1),
        footprints.reshape(SIDE, SIDE, comps),
        traces.reshape(comps, frames),
        centre_row,
        centre_col,
        radius,
        comp_count,
        tables,
    )
    return (new_foot.reshape(1, SIDE * SIDE, comps), new_trace[None])


def solution(mesh):
    in_specs = (
        P(("groups", "tile"), None, "tm"),
        P(("groups", "tile"), None, None),
        P(("groups", "tile"), None, None),
        P(("groups", "tile"), None, "tm"),
        P(("groups", "tile"), None),
        P(("groups", "tile"), None),
        P(("groups", "tile"), None),
        P(("groups", "tile")),
    )
    out_specs = (P(("groups", "tile"), None, None), P(("groups", "tile"), None, "tm"))
    return jax.shard_map(shards, mesh=mesh, in_specs=in_specs, out_specs=out_specs, check_vma=False)
```

time: 275 us -> 66.1 us (0.24)
  the two profiles are of different devices: /device:TPU:0 before, /device:TPU:26 now
where the time goes in v1:
time: 66.1 us; the launch traced here: 65.9 us
  Pallas kernels  59 us (89%)
  local copies, waits for them, and re-layouts  5.67 us (9%)
  between operations  1.29 us (2%)
    pallas_call x1, Pallas kernels, shards(): pl.pallas_call(functools.partial(kernel, n, s, shares), out_shape=(jax.Sh...  59 us
    unnamed x5, local copies, waits for them, and re-layouts  5.67 us

profile of v1, /device:TPU:26, one launch (start us, length us, event | category | flops | bytes accessed | tf_op | source)
XLA Modules:
  0.0 65.9 jit_solution(7202018951144105982)
XLA Ops:
  1.3 2.0 %copy.11 = bf16[1,2304,56]{2,1,0:T(8,128)(2,1)} copy(bf16[1,2304,56]{1,2,0:T(8,128)(2,1)} %param.10) | data formatting | bytes 516096 | tf_op args[1]
  3.3 59.0 %shard_map.104 = (bf16[48,48,384]{2,1,0:T(8,128)(2,1)}, bf16[384,512]{1,0:T(8,128)(2,1)}) custom-call(bf16[48,48,512]{2,1,0:T(8,128)(2,1)} %bitcast.7, bf16[48,48,56]{2,1,0:T(8,128)(2,1)} %bitcast.6, bf16[48,48,384]{2,1,0:T(8,128)(2,1)} %bitcast.8, bf16[384,512]{1,0:T(8,128)(2,1)} %bitcast.10, s32[1,384]{1,0:T(1,128)} %row_at.1, s32[1,384]{1,0:T(1,128)} %col_at.1, ...), custom_call_target="tpu_custom_call" | custom-call | tf_op jit(solution)/shard_map/pallas_call | solution.py:314
  62.3 0.0 copy-start
  62.3 2.9 %copy.15 = bf16[1,2304,384]{2,1,0:T(8,128)(2,1)} copy(bf16[1,2304,384]{2,1,0:T(8,128)(2,1)} %bitcast.9) | data formatting | bytes 3538944
  65.2 0.0 copy-done
  65.2 0.7 %copy.16 = bf16[1,384,512]{2,1,0:T(8,128)(2,1)} copy(bf16[1,384,512]{2,1,0:T(8,128)(2,1)S(1)} %bitcast.11) | data formatting | bytes 786432
Async XLA Ops:
  62.3 2.9 %copy-start = (bf16[384,512]{1,0:T(8,128)(2,1)S(1)}, bf16[384,512]{1,0:T(8,128)(2,1)}, u32[]{:S(2)}) copy-start(bf16[384,512]{1,0:T(8,128)(2,1)} %get-tuple-element.5) | copy-start | bytes 1179652

commit v2 on v1

--- a/solution.py
+++ b/solution.py
@@ -11,10 +11,13 @@
 SIDE = 48
 CYCLE = 8
 WIDE = SIDE + 2 * CYCLE
+FOLD_ROWS = 16
 FOLD = 24
+HALF = FOLD // 2
 PASSES = 2
 RIDGE_TERM = 1.0
-BLOCK = 4
+BLOCK = 8
+DEPTH = 16
 SPAN = BLOCK + 2 * CYCLE
 LANES = 128
 F32 = jnp.float32
@@ -42,15 +45,21 @@
     return tables
 
 
-def fold_columns(rows):
-    return rows[:, :FOLD] + rows[:, FOLD:]
+def swap_halves(rows):
+    return jnp.concatenate([rows[:, HALF:], rows[:, :HALF]], axis=1)
+
+
+def fold(rows, s):
+    rows = rows[:, :FOLD] + rows[:, FOLD:]
+    rows = rows[:s] + swap_halves(rows[s : 2 * s]) + rows[2 * s :]
+    return rows.reshape(s * FOLD, rows.shape[2])
 
 
 def kernel(
     n, s, shares,
-    movie, weights, prints, traces, row_at, col_at, reach, count, tables,
+    movie, stored, prints, traces, row_at, col_at, reach, count, tables,
     new_foot, new_trace,
-    foot, band, pm, win, errs, backs, trace, gacc, inv_den, col_sq,
+    weights, foot, band, pm, win, errs, backs, trace, gacc, inv_den, col_sq,
     halo_out, halo_in, part, own, arrived, energy_out, energy_in, gathered,
     halo_sems, part_sems, energy_sems, gather_sems,
 ):
@@ -89,8 +98,10 @@
     for q in range(frames // LANES):
         cols = slice(q * LANES, (q + 1) * LANES)
         trace[:, cols] = jnp.where(live, traces[:, cols].astype(F32), 0.0).astype(BF16)
-    win[0:CYCLE] = jnp.zeros((CYCLE, WIDE, frames), BF16)
-    win[CYCLE + SIDE : WIDE] = jnp.zeros((CYCLE, WIDE, frames), BF16)
+    pixels = BLOCK * SIDE
+    for b in range(blocks):
+        turned = jnp.transpose(stored[:, b * pixels : (b + 1) * pixels].astype(F32))
+        weights[b * BLOCK : (b + 1) * BLOCK] = turned.astype(BF16).reshape(BLOCK, SIDE, -1)
     pl.semaphore_wait(barrier, n)
 
     def halo_copy(sweep):
@@ -123,17 +134,18 @@
     for sweep in range(PASSES):
 
         def residual(b, carry):
-            rows = pl.ds(b * BLOCK, BLOCK)
+            rows = pl.ds(b * DEPTH, DEPTH)
             prod = jnp.dot(
-                foot[rows].reshape(BLOCK * SIDE, comps), trace[...], preferred_element_type=F32
+                foot[rows].reshape(DEPTH * SIDE, comps), trace[...], preferred_element_type=F32
             )
-            diff = prod.reshape(BLOCK, SIDE, frames) - movie[rows].astype(F32)
+            diff = prod.reshape(DEPTH, SIDE, frames) - movie[rows].astype(F32)
             pm[rows] = diff
             edge = jnp.where(tile == 0, -diff[:, SIDE - CYCLE :], -diff[:, :CYCLE])
-            halo_out[sweep, b] = edge.reshape(BLOCK * CYCLE, frames).astype(BF16)
+            edge = edge.reshape(DEPTH * CYCLE, frames).astype(BF16)
+            halo_out[sweep, pl.ds(b * DEPTH * CYCLE, DEPTH * CYCLE)] = edge
             return carry
 
-        lax.fori_loop(0, blocks, residual, 0)
+        lax.fori_loop(0, SIDE // DEPTH, residual, 0)
         copy = halo_copy(sweep)
         copy.start()
         if sweep == 0:
@@ -142,41 +154,41 @@
 
         def fill(b, carry):
             rows = pl.ds(b * BLOCK, BLOCK)
-            edge = halo_in[sweep, b].astype(F32).reshape(BLOCK, CYCLE, frames)
+            edge = halo_in[sweep, pl.ds(b * BLOCK * CYCLE, BLOCK * CYCLE)]
+            edge = edge.astype(F32).reshape(BLOCK, CYCLE, frames)
             low = jnp.where(tile == 0, 0.0, edge)
             high = jnp.where(tile == 0, edge, 0.0)
             whole = jnp.concatenate([low, -pm[rows], high], axis=1)
-            win[pl.ds(CYCLE + b * BLOCK, BLOCK)] = whole.astype(BF16)
+            win[rows] = whole.astype(BF16)
             return carry
 
         lax.fori_loop(0, blocks, fill, 0)
 
-        def background(b, carry):
-            rows = pl.ds(b * BLOCK, BLOCK)
-            seen = win[pl.ds(b * BLOCK, SPAN)].reshape(SPAN * WIDE, frames)
-            back = jnp.dot(band[b], seen, preferred_element_type=F32).astype(BF16)
+        for b in range(blocks):
+            rows = slice(b * BLOCK, (b + 1) * BLOCK)
+            first = b * BLOCK - CYCLE
+            low, high = max(first, 0), min(first + SPAN, SIDE)
+            seen = win[low:high].reshape((high - low) * WIDE, frames)
+            taps = band[b, :, (low - first) * WIDE : (high - first) * WIDE]
+            back = jnp.dot(taps, seen, preferred_element_type=F32).astype(BF16)
             back = back.reshape(BLOCK, SIDE, frames)
             if sweep == PASSES - 1:
                 backs[rows] = back
             errs[rows] = (pm[rows] + back.astype(F32)).astype(BF16)
-            return carry
-
-        lax.fori_loop(0, blocks, background, 0)
-
-        depth = 16
+
         gacc[...] = jnp.zeros_like(gacc)
 
         def descend(j, carry):
-            rows = pl.ds(j * depth, depth)
+            rows = pl.ds(j * DEPTH, DEPTH)
             gacc[...] += lax.dot_general(
-                foot[rows].reshape(depth * SIDE, comps),
-                errs[rows].reshape(depth * SIDE, frames),
+                foot[rows].reshape(DEPTH * SIDE, comps),
+                errs[rows].reshape(DEPTH * SIDE, frames),
                 (((0,), (0,)), ((), ())),
                 preferred_element_type=F32,
             )
             return carry
 
-        lax.fori_loop(0, SIDE // depth, descend, 0)
+        lax.fori_loop(0, SIDE // DEPTH, descend, 0)
         for q in range(frames // LANES):
             cols = slice(q * LANES, (q + 1) * LANES)
             moved = jnp.maximum(trace[:, cols].astype(F32) - gacc[:, cols] * inv_den[...], 0.0)
@@ -235,18 +247,21 @@
 
     over_peers(lambda peer: owns(peer, lambda: energy_copy(peer, me).start()))
 
+    def rows_of(ref, share):
+        return [ref[pl.ds(a * FOLD_ROWS + share * s, s)] for a in range(SIDE // FOLD_ROWS)]
+
     def share_of(share):
-        top, low = pl.ds(share * s, s), pl.ds(FOLD + share * s, s)
-        feet = jnp.concatenate([foot[top], foot[low]], axis=0).reshape(2 * s * SIDE, comps)
+        held = SIDE // FOLD_ROWS * s * SIDE
+        feet = jnp.concatenate(rows_of(foot, share), axis=0).reshape(held, comps)
         prod = jnp.dot(feet, trace[...], preferred_element_type=F32)
-        back = jnp.concatenate([backs[top], backs[low]], axis=0).reshape(2 * s * SIDE, frames)
-        seen = jnp.concatenate([movie[top], movie[low]], axis=0).reshape(2 * s * SIDE, frames)
+        back = jnp.concatenate(rows_of(backs, share), axis=0).reshape(held, frames)
+        seen = jnp.concatenate(rows_of(movie, share), axis=0).reshape(held, frames)
         ferr = (prod + back.astype(F32) - seen.astype(F32)).astype(BF16)
         grad = lax.dot_general(
             ferr, trace[...], (((1,), (1,)), ((), ())), preferred_element_type=F32
         )
-        grad = jnp.where(feet.astype(F32) > 0.0, grad, 0.0).reshape(2 * s, SIDE, comps)
-        return fold_columns(grad[:s] + grad[s:]).reshape(s * FOLD, comps)
+        grad = jnp.where(feet.astype(F32) > 0.0, grad, 0.0)
+        return fold(grad.reshape(held // SIDE, SIDE, comps), s)
 
     def send_share(share):
         part[share] = share_of(share).astype(BF16)
@@ -266,8 +281,7 @@
 
         over_peers(take)
         den_c = energy_in[me][:1] + RIDGE_TERM
-        top, low = pl.ds(me * s, s), pl.ds(FOLD + me * s, s)
-        feet = fold_columns(foot[top].astype(F32) + foot[low].astype(F32)).reshape(s * FOLD, comps)
+        feet = fold(jnp.concatenate(rows_of(foot, me), axis=0).astype(F32), s)
         gathered[me] = jnp.maximum(feet - own[...] / den_c, 0.0).astype(BF16)
         over_peers(lambda peer: gather_copy(peer, me).start())
 
@@ -275,10 +289,12 @@
 
     def unfold(share):
         values = gathered[share].astype(F32).reshape(s, FOLD, comps)
+        turned = swap_halves(values)
         values = jnp.concatenate([values, values], axis=1)
-        for half in range(2):
-            rows = pl.ds(half * FOLD + share * s, s)
-            new_foot[rows] = jnp.where(foot[rows].astype(F32) > 0.0, values, 0.0).astype(BF16)
+        turned = jnp.concatenate([turned, turned], axis=1)
+        for a in range(SIDE // FOLD_ROWS):
+            rows = pl.ds(a * FOLD_ROWS + share * s, s)
+            new_foot[rows] = jnp.where(foot[rows].astype(F32) > 0.0, (values, turned)[a % 2], 0.0).astype(BF16)
 
     owns(me, lambda: unfold(me))
 
@@ -303,10 +319,10 @@
     n = lax.axis_size("tm")
     frames = movie.shape[2]
     comps = footprints.shape[2]
-    s = -(-FOLD // n)
-    while FOLD % s:
+    s = -(-FOLD_ROWS // n)
+    while FOLD_ROWS % s:
         s += 1
-    shares = FOLD // s
+    shares = FOLD_ROWS // s
     blocks = SIDE // BLOCK
     tables = jnp.asarray(spread_tables(), BF16)
     vmem = pl.BlockSpec(memory_space=pltpu.VMEM)
@@ -320,18 +336,19 @@
         in_specs=[vmem] * 7 + [smem, vmem],
         out_specs=(vmem, vmem),
         scratch_shapes=[
+            pltpu.VMEM((SIDE, SIDE, cycle_weights.shape[2]), BF16),
             pltpu.VMEM((SIDE, SIDE, comps), BF16),
             pltpu.VMEM((blocks, BLOCK * SIDE, SPAN * WIDE), BF16),
             pltpu.VMEM((SIDE, SIDE, frames), F32),
-            pltpu.VMEM((WIDE, WIDE, frames), BF16),
+            pltpu.VMEM((SIDE, WIDE, frames), BF16),
             pltpu.VMEM((SIDE, SIDE, frames), BF16),
             pltpu.VMEM((SIDE, SIDE, frames), BF16),
             pltpu.VMEM((comps, frames), BF16),
             pltpu.VMEM((comps, frames), F32),
             pltpu.VMEM((comps, LANES), F32),
             pltpu.VMEM((SIDE, comps), jnp.int32),
-            pltpu.VMEM((PASSES, blocks, BLOCK * CYCLE, frames), BF16),
-            pltpu.VMEM((PASSES, blocks, BLOCK * CYCLE, frames), BF16),
+            pltpu.VMEM((PASSES, SIDE * CYCLE, frames), BF16),
+            pltpu.VMEM((PASSES, SIDE * CYCLE, frames), BF16),
             pltpu.VMEM((n, s * FOLD, comps), BF16),
             pltpu.VMEM((s * FOLD, comps), F32),
             pltpu.VMEM((n, s * FOLD, comps), BF16),
@@ -348,7 +365,7 @@
         ),
     )(
         movie.reshape(SIDE, SIDE, frames),
-        cycle_weights.reshape(SIDE, SIDE, -1),
+        jnp.transpose(cycle_weights[0]),
         footprints.reshape(SIDE, SIDE, comps),
         traces.reshape(comps, frames),
         centre_row,

time: 66.1 us -> 50.2 us (0.76)
  the two profiles are of different devices: /device:TPU:26 before, /device:TPU:0 now
where the time goes in v2:
time: 50.2 us; the launch traced here: 50 us
  Pallas kernels  45.1 us (90%)
  local copies, waits for them, and re-layouts  3.66 us (7%)
  between operations  1.3 us (3%)
    pallas_call x1, Pallas kernels, shards(): pl.pallas_call(functools.partial(kernel, n, s, shares), out_shape=(jax.Sh...  45.1 us
    unnamed x4, local copies, waits for them, and re-layouts  3.66 us

profile of v2, /device:TPU:0, one launch (start us, length us, event | category | flops | bytes accessed | tf_op | source)
XLA Modules:
  0.0 50.0 jit_solution(2974478827837260191)
XLA Ops:
  1.3 45.1 %shard_map.104 = (bf16[48,48,384]{2,1,0:T(8,128)(2,1)}, bf16[384,512]{1,0:T(8,128)(2,1)}) custom-call(bf16[48,48,512]{2,1,0:T(8,128)(2,1)} %bitcast.8, bf16[56,2304]{1,0:T(8,128)(2,1)} %bitcast.13, bf16[48,48,384]{2,1,0:T(8,128)(2,1)} %bitcast.9, bf16[384,512]{1,0:T(8,128)(2,1)} %bitcast.11, s32[1,384]{1,0:T(1,128)} %row_at.1, s32[1,384]{1,0:T(1,128)} %col_at.1, ...), custom_call_target="tpu_custom_call" | custom-call | tf_op jit(solution)/shard_map/pallas_call | solution.py:330
  46.4 0.0 copy-start
  46.4 2.9 %copy.14 = bf16[1,2304,384]{2,1,0:T(8,128)(2,1)} copy(bf16[1,2304,384]{2,1,0:T(8,128)(2,1)} %bitcast.10) | data formatting | bytes 3538944
  49.3 0.0 copy-done
  49.3 0.7 %copy.15 = bf16[1,384,512]{2,1,0:T(8,128)(2,1)} copy(bf16[1,384,512]{2,1,0:T(8,128)(2,1)S(1)} %bitcast.12) | data formatting | bytes 786432
Async XLA Ops:
  46.4 2.9 %copy-start = (bf16[384,512]{1,0:T(8,128)(2,1)S(1)}, bf16[384,512]{1,0:T(8,128)(2,1)}, u32[]{:S(2)}) copy-start(bf16[384,512]{1,0:T(8,128)(2,1)} %get-tuple-element.5) | copy-start | bytes 1179652

commit v3 on v2

--- a/solution.py
+++ b/solution.py
@@ -56,12 +56,12 @@
 
 
 def kernel(
-    n, s, shares,
+    n, s,
     movie, stored, prints, traces, row_at, col_at, reach, count, tables,
-    new_foot, new_trace,
-    weights, foot, band, pm, win, errs, backs, trace, gacc, inv_den, col_sq,
+    foot_out, trace_out, packed_out,
+    feet_edge, seen_edge, weights, foot, band, pm, win, errs, backs, trace, gacc, inv_den, col_sq,
     halo_out, halo_in, part, own, arrived, energy_out, energy_in, gathered,
-    halo_sems, part_sems, energy_sems, gather_sems,
+    halo_sems, part_sems, energy_sems, gather_sems, relay_sems, out_sems, share_sems,
 ):
     me = lax.axis_index("tm")
     tile = lax.axis_index("tile")
@@ -98,6 +98,17 @@
     for q in range(frames // LANES):
         cols = slice(q * LANES, (q + 1) * LANES)
         trace[:, cols] = jnp.where(live, traces[:, cols].astype(F32), 0.0).astype(BF16)
+
+    def cut_edge(j, carry):
+        rows = pl.ds(j * DEPTH, DEPTH)
+        spots = pl.ds(j * DEPTH * CYCLE, DEPTH * CYCLE)
+        for ref, edge in ((foot, feet_edge), (movie, seen_edge)):
+            whole = ref[rows].astype(F32)
+            cut = jnp.where(tile == 0, whole[:, SIDE - CYCLE :], whole[:, :CYCLE])
+            edge[spots] = cut.reshape(DEPTH * CYCLE, ref.shape[2]).astype(BF16)
+        return carry
+
+    lax.fori_loop(0, SIDE // DEPTH, cut_edge, 0)
     pixels = BLOCK * SIDE
     for b in range(blocks):
         turned = jnp.transpose(stored[:, b * pixels : (b + 1) * pixels].astype(F32))
@@ -131,6 +142,9 @@
                 band[b, rows, last:] = jnp.zeros((SIDE, SPAN * WIDE - last), BF16)
         return carry
 
+    foot_copy = pltpu.make_async_copy(foot, foot_out, out_sems.at[0])
+    trace_copy = pltpu.make_async_copy(trace, trace_out, out_sems.at[1])
+
     for sweep in range(PASSES):
 
         def residual(b, carry):
@@ -140,16 +154,16 @@
             )
             diff = prod.reshape(DEPTH, SIDE, frames) - movie[rows].astype(F32)
             pm[rows] = diff
-            edge = jnp.where(tile == 0, -diff[:, SIDE - CYCLE :], -diff[:, :CYCLE])
-            edge = edge.reshape(DEPTH * CYCLE, frames).astype(BF16)
-            halo_out[sweep, pl.ds(b * DEPTH * CYCLE, DEPTH * CYCLE)] = edge
             return carry
 
-        lax.fori_loop(0, SIDE // DEPTH, residual, 0)
+        ahead = jnp.dot(feet_edge[...], trace[...], preferred_element_type=F32)
+        halo_out[sweep] = (seen_edge[...].astype(F32) - ahead).astype(BF16)
         copy = halo_copy(sweep)
         copy.start()
+        lax.fori_loop(0, SIDE // DEPTH, residual, 0)
         if sweep == 0:
             lax.fori_loop(0, blocks, build_band, 0)
+            foot_copy.start()
         copy.wait_recv()
 
         def fill(b, carry):
@@ -194,7 +208,6 @@
             moved = jnp.maximum(trace[:, cols].astype(F32) - gacc[:, cols] * inv_den[...], 0.0)
             trace[:, cols] = jnp.where(live, moved, 0.0).astype(BF16)
 
-    new_trace[...] = trace[...]
     squares = jnp.zeros((comps, LANES), F32)
     for q in range(frames // LANES):
         now = trace[:, q * LANES : (q + 1) * LANES].astype(F32)
@@ -232,11 +245,28 @@
             device_id_type=MESH,
         )
 
-    def owns(index, do):
-        if shares == n:
-            do()
-        else:
-            pl.when(index < shares)(do)
+    bit, pair, pairs = lax.rem(me, 2), me // 2, n // 2
+    partner = me + 1 - 2 * bit
+
+    def relay_copy(share):
+        return pltpu.make_async_remote_copy(
+            src_ref=gathered.at[share],
+            dst_ref=gathered.at[share],
+            send_sem=relay_sems.at[share],
+            recv_sem=gather_sems.at[1, share],
+            device_id={"tm": partner},
+            device_id_type=MESH,
+        )
+
+    def share_copy(share):
+        return pltpu.make_async_copy(gathered.at[share], packed_out.at[share], share_sems.at[share])
+
+    def over_pairs(do, way=1):
+        def step(t, carry):
+            do(lax.rem(pair + (1 + t if way == 1 else pairs - 1 - t), pairs))
+            return carry
+
+        lax.fori_loop(0, pairs - 1, step, 0)
 
     def over_peers(do):
         def step(t, carry):
@@ -245,7 +275,7 @@
 
         lax.fori_loop(0, n - 1, step, 0)
 
-    over_peers(lambda peer: owns(peer, lambda: energy_copy(peer, me).start()))
+    over_peers(lambda peer: energy_copy(peer, me).start())
 
     def rows_of(ref, share):
         return [ref[pl.ds(a * FOLD_ROWS + share * s, s)] for a in range(SIDE // FOLD_ROWS)]
@@ -267,75 +297,91 @@
         part[share] = share_of(share).astype(BF16)
         part_copy(share, me).start()
 
-    over_peers(lambda peer: owns(peer, lambda: send_share(peer)))
-
-    def settle():
-        own[...] = share_of(me)
-        energy_in[me] = energy_out[...]
-
-        def take(peer):
-            energy_copy(me, peer).wait_recv()
-            part_copy(me, peer).wait_recv()
-            own[...] += arrived[peer].astype(F32)
-            energy_in[me] += energy_in[peer]
-
-        over_peers(take)
-        den_c = energy_in[me][:1] + RIDGE_TERM
-        feet = fold(jnp.concatenate(rows_of(foot, me), axis=0).astype(F32), s)
-        gathered[me] = jnp.maximum(feet - own[...] / den_c, 0.0).astype(BF16)
-        over_peers(lambda peer: gather_copy(peer, me).start())
-
-    owns(me, settle)
-
-    def unfold(share):
-        values = gathered[share].astype(F32).reshape(s, FOLD, comps)
-        turned = swap_halves(values)
-        values = jnp.concatenate([values, values], axis=1)
-        turned = jnp.concatenate([turned, turned], axis=1)
-        for a in range(SIDE // FOLD_ROWS):
-            rows = pl.ds(a * FOLD_ROWS + share * s, s)
-            new_foot[rows] = jnp.where(foot[rows].astype(F32) > 0.0, (values, turned)[a % 2], 0.0).astype(BF16)
-
-    owns(me, lambda: unfold(me))
-
-    def receive(peer):
-        gather_copy(me, peer).wait_recv()
-        unfold(peer)
-
-    over_peers(lambda peer: owns(peer, lambda: receive(peer)))
+    over_peers(send_share)
+    trace_copy.start()
+
+    own[...] = share_of(me)
+    energy_in[me] = energy_out[...]
+
+    def take(peer):
+        energy_copy(me, peer).wait_recv()
+        part_copy(me, peer).wait_recv()
+        own[...] += arrived[peer].astype(F32)
+        energy_in[me] += energy_in[peer]
+
+    over_peers(take)
+    den_c = energy_in[me][:1] + RIDGE_TERM
+    feet = fold(jnp.concatenate(rows_of(foot, me), axis=0).astype(F32), s)
+    gathered[me] = jnp.maximum(feet - own[...] / den_c, 0.0).astype(BF16)
+    gather_copy(partner, me).start()
+    over_pairs(lambda other: gather_copy(2 * other + bit, me).start())
+    share_copy(me).start()
+
+    def relay(other):
+        share = 2 * other + bit
+        gather_copy(me, share).wait_recv()
+        relay_copy(share).start()
+        share_copy(share).start()
+
+    def receive(share):
+        gather_copy(me, share).wait_recv()
+        share_copy(share).start()
+
+    over_pairs(relay, -1)
+    receive(partner)
+    over_pairs(lambda other: receive(2 * other + 1 - bit), -1)
 
     for sweep in range(PASSES):
         halo_copy(sweep).wait_send()
+    foot_copy.wait()
+    trace_copy.wait()
 
     def drain(peer):
-        owns(peer, lambda: energy_copy(peer, me).wait_send())
-        owns(peer, lambda: part_copy(peer, me).wait_send())
-        owns(me, lambda: gather_copy(peer, me).wait_send())
+        energy_copy(peer, me).wait_send()
+        part_copy(peer, me).wait_send()
+        share_copy(peer).wait()
+
+    def drain_pair(other):
+        gather_copy(2 * other + bit, me).wait_send()
+        relay_copy(2 * other + bit).wait_send()
 
     over_peers(drain)
+    over_pairs(drain_pair)
+    gather_copy(partner, me).wait_send()
+    share_copy(me).wait()
+
+
+def spread(packed, foot, trace, new_foot, new_trace):
+    values = packed[...].astype(F32)
+    values = jnp.where(pl.program_id(0) % 2 == 1, swap_halves(values), values)
+    values = jnp.concatenate([values, values], axis=1)
+    new_foot[...] = jnp.where(foot[...].astype(F32) > 0.0, values, 0.0).astype(BF16)
+    new_trace[...] = trace[...]
 
 
 def shards(movie, cycle_weights, footprints, traces, centre_row, centre_col, radius, comp_count):
     n = lax.axis_size("tm")
     frames = movie.shape[2]
     comps = footprints.shape[2]
-    s = -(-FOLD_ROWS // n)
-    while FOLD_ROWS % s:
-        s += 1
-    shares = FOLD_ROWS // s
+    assert n % 2 == 0 and FOLD_ROWS % n == 0
+    s = FOLD_ROWS // n
     blocks = SIDE // BLOCK
     tables = jnp.asarray(spread_tables(), BF16)
     vmem = pl.BlockSpec(memory_space=pltpu.VMEM)
     smem = pl.BlockSpec(memory_space=pltpu.SMEM)
-    new_foot, new_trace = pl.pallas_call(
-        functools.partial(kernel, n, s, shares),
+    hbm = pl.BlockSpec(memory_space=pl.ANY)
+    foot, trace, packed = pl.pallas_call(
+        functools.partial(kernel, n, s),
         out_shape=(
             jax.ShapeDtypeStruct((SIDE, SIDE, comps), BF16),
             jax.ShapeDtypeStruct((comps, frames), BF16),
+            jax.ShapeDtypeStruct((n, s * FOLD, comps), BF16),
         ),
         in_specs=[vmem] * 7 + [smem, vmem],
-        out_specs=(vmem, vmem),
+        out_specs=(hbm, hbm, hbm),
         scratch_shapes=[
+            pltpu.VMEM((SIDE * CYCLE, comps), BF16),
+            pltpu.VMEM((SIDE * CYCLE, frames), BF16),
             pltpu.VMEM((SIDE, SIDE, cycle_weights.shape[2]), BF16),
             pltpu.VMEM((SIDE, SIDE, comps), BF16),
             pltpu.VMEM((blocks, BLOCK * SIDE, SPAN * WIDE), BF16),
@@ -359,6 +405,9 @@
             pltpu.SemaphoreType.DMA((2, n)),
             pltpu.SemaphoreType.DMA((2, n)),
             pltpu.SemaphoreType.DMA((2, n)),
+            pltpu.SemaphoreType.DMA((n,)),
+            pltpu.SemaphoreType.DMA((2,)),
+            pltpu.SemaphoreType.DMA((n,)),
         ],
         compiler_params=pltpu.CompilerParams(
             collective_id=0, has_side_effects=True, vmem_limit_bytes=60 * 1024 * 1024
@@ -374,6 +423,20 @@
         comp_count,
         tables,
     )
+    steps = SIDE // FOLD_ROWS
+    rows = pl.BlockSpec((FOLD_ROWS, SIDE, comps), lambda a: (a, 0, 0))
+    parts = pl.BlockSpec((comps // steps, frames), lambda a: (a, 0))
+    new_foot, new_trace = pl.pallas_call(
+        spread,
+        grid=(steps,),
+        out_shape=(
+            jax.ShapeDtypeStruct((SIDE, SIDE, comps), BF16),
+            jax.ShapeDtypeStruct((comps, frames), BF16),
+        ),
+        in_specs=[pl.BlockSpec((FOLD_ROWS, FOLD, comps), lambda a: (0, 0, 0)), rows, parts],
+        out_specs=(rows, parts),
+        compiler_params=pltpu.CompilerParams(vmem_limit_bytes=60 * 1024 * 1024),
+    )(packed.reshape(FOLD_ROWS, FOLD, comps), foot, trace)
     return (new_foot.reshape(1, SIDE * SIDE, comps), new_trace[None])
 
 

time: 50.2 us -> 52.8 us (1.052)
  Pallas kernels: 45.1 us -> 51.3 us
  local copies, waits for them, and re-layouts: 3.66 us -> 0 us
    pallas_call x1 -> x2, Pallas kernels: 45.1 us -> 51.3 us  [the longest x1 47.1 us: shards(): pl.pallas_call(functools.partial(kernel, n, s), out_shape=(jax.ShapeDtype...]
    unnamed x4 -> x0, local copies, waits for them, and re-layouts: 3.66 us -> none
where the time goes in v3:
time: 52.8 us; the launch traced here: 52.6 us
  Pallas kernels  51.3 us (97%)
  between operations  1.29 us (2%)
    pallas_call x1, Pallas kernels, shards(): pl.pallas_call(functools.partial(kernel, n, s), out_shape=(jax.ShapeDtype...  47.1 us
    pallas_call x1, Pallas kernels, shards(): pl.pallas_call(spread, grid=(steps,), out_shape=(jax.ShapeDtypeStruct((SI...  4.2 us

profile of v3, /device:TPU:0, one launch (start us, length us, event | category | flops | bytes accessed | tf_op | source)
XLA Modules:
  0.0 52.6 jit_solution(9609187092546142672)
XLA Ops:
  1.3 47.1 %shard_map.104 = (bf16[48,48,384]{2,1,0:T(8,128)(2,1)}, bf16[384,512]{1,0:T(8,128)(2,1)}, bf16[8,48,384]{2,1,0:T(8,128)(2,1)}) custom-call(bf16[48,48,512]{2,1,0:T(8,128)(2,1)} %bitcast.9, bf16[56,2304]{1,0:T(8,128)(2,1)} %bitcast.13, bf16[48,48,384]{2,1,0:T(8,128)(2,1)} %bitcast.10, bf16[384,512]{1,0:T(8,128)(2,1)} %bitcast.11, s32[1,384]{1,0:T(1,128)} %row_at.1, ...), custom_call_target="tpu_custom_call" | custom-call | tf_op jit(solution)/shard_map/pallas_call | solution.py:373
  48.4 4.2 %shard_map.105 = (bf16[48,48,384]{2,1,0:T(8,128)(2,1)}, bf16[384,512]{1,0:T(8,128)(2,1)}) custom-call(bf16[16,24,384]{2,1,0:T(8,128)(2,1)} %bitcast.12, bf16[48,48,384]{2,1,0:T(8,128)(2,1)} %get-tuple-element.8.foot, bf16[384,512]{1,0:T(8,128)(2,1)} %get-tuple-element.9.trace), custom_call_target="tpu_custom_call" | custom-call | tf_op jit(solution)/shard_map/pallas_call | solution.py:429

commit v4 on v2

--- a/solution.py
+++ b/solution.py
@@ -59,7 +59,7 @@
     n, s, shares,
     movie, stored, prints, traces, row_at, col_at, reach, count, tables,
     new_foot, new_trace,
-    weights, foot, band, pm, win, errs, backs, trace, gacc, inv_den, col_sq,
+    feet_edge, seen_edge, weights, foot, band, pm, win, errs, backs, trace, gacc, inv_den, col_sq,
     halo_out, halo_in, part, own, arrived, energy_out, energy_in, gathered,
     halo_sems, part_sems, energy_sems, gather_sems,
 ):
@@ -98,6 +98,17 @@
     for q in range(frames // LANES):
         cols = slice(q * LANES, (q + 1) * LANES)
         trace[:, cols] = jnp.where(live, traces[:, cols].astype(F32), 0.0).astype(BF16)
+
+    def cut_edge(j, carry):
+        rows = pl.ds(j * DEPTH, DEPTH)
+        spots = pl.ds(j * DEPTH * CYCLE, DEPTH * CYCLE)
+        for ref, edge in ((foot, feet_edge), (movie, seen_edge)):
+            whole = ref[rows].astype(F32)
+            cut = jnp.where(tile == 0, whole[:, SIDE - CYCLE :], whole[:, :CYCLE])
+            edge[spots] = cut.reshape(DEPTH * CYCLE, ref.shape[2]).astype(BF16)
+        return carry
+
+    lax.fori_loop(0, SIDE // DEPTH, cut_edge, 0)
     pixels = BLOCK * SIDE
     for b in range(blocks):
         turned = jnp.transpose(stored[:, b * pixels : (b + 1) * pixels].astype(F32))
@@ -140,14 +151,13 @@
             )
             diff = prod.reshape(DEPTH, SIDE, frames) - movie[rows].astype(F32)
             pm[rows] = diff
-            edge = jnp.where(tile == 0, -diff[:, SIDE - CYCLE :], -diff[:, :CYCLE])
-            edge = edge.reshape(DEPTH * CYCLE, frames).astype(BF16)
-            halo_out[sweep, pl.ds(b * DEPTH * CYCLE, DEPTH * CYCLE)] = edge
             return carry
 
-        lax.fori_loop(0, SIDE // DEPTH, residual, 0)
+        ahead = jnp.dot(feet_edge[...], trace[...], preferred_element_type=F32)
+        halo_out[sweep] = (seen_edge[...].astype(F32) - ahead).astype(BF16)
         copy = halo_copy(sweep)
         copy.start()
+        lax.fori_loop(0, SIDE // DEPTH, residual, 0)
         if sweep == 0:
             lax.fori_loop(0, blocks, build_band, 0)
         copy.wait_recv()
@@ -336,6 +346,8 @@
         in_specs=[vmem] * 7 + [smem, vmem],
         out_specs=(vmem, vmem),
         scratch_shapes=[
+            pltpu.VMEM((SIDE * CYCLE, comps), BF16),
+            pltpu.VMEM((SIDE * CYCLE, frames), BF16),
             pltpu.VMEM((SIDE, SIDE, cycle_weights.shape[2]), BF16),
             pltpu.VMEM((SIDE, SIDE, comps), BF16),
             pltpu.VMEM((blocks, BLOCK * SIDE, SPAN * WIDE), BF16),

time: 50.2 us -> 49.6 us (0.988)
  Pallas kernels: 45.1 us -> 44.5 us
    pallas_call x1, Pallas kernels: 45.1 us -> 44.5 us  [shards(): pl.pallas_call(functools.partial(kernel, n, s, shares), out_shape=(jax.Sh...]
where the time goes in v4:
time: 49.6 us; the launch traced here: 49.4 us
  Pallas kernels  44.5 us (90%)
  local copies, waits for them, and re-layouts  3.66 us (7%)
  between operations  1.3 us (3%)
    pallas_call x1, Pallas kernels, shards(): pl.pallas_call(functools.partial(kernel, n, s, shares), out_shape=(jax.Sh...  44.5 us
    unnamed x4, local copies, waits for them, and re-layouts  3.66 us

profile of v4, /device:TPU:0, one launch (start us, length us, event | category | flops | bytes accessed | tf_op | source)
XLA Modules:
  0.0 49.4 jit_solution(12698685167578294875)
XLA Ops:
  1.3 44.5 %shard_map.104 = (bf16[48,48,384]{2,1,0:T(8,128)(2,1)}, bf16[384,512]{1,0:T(8,128)(2,1)}) custom-call(bf16[48,48,512]{2,1,0:T(8,128)(2,1)} %bitcast.8, bf16[56,2304]{1,0:T(8,128)(2,1)} %bitcast.13, bf16[48,48,384]{2,1,0:T(8,128)(2,1)} %bitcast.9, bf16[384,512]{1,0:T(8,128)(2,1)} %bitcast.11, s32[1,384]{1,0:T(1,128)} %row_at.1, s32[1,384]{1,0:T(1,128)} %col_at.1, ...), custom_call_target="tpu_custom_call" | custom-call | tf_op jit(solution)/shard_map/pallas_call | solution.py:340
  45.8 0.0 copy-start
  45.8 2.9 %copy.14 = bf16[1,2304,384]{2,1,0:T(8,128)(2,1)} copy(bf16[1,2304,384]{2,1,0:T(8,128)(2,1)} %bitcast.10) | data formatting | bytes 3538944
  48.7 0.0 copy-done
  48.7 0.7 %copy.15 = bf16[1,384,512]{2,1,0:T(8,128)(2,1)} copy(bf16[1,384,512]{2,1,0:T(8,128)(2,1)S(1)} %bitcast.12) | data formatting | bytes 786432
Async XLA Ops:
  45.8 2.9 %copy-start = (bf16[384,512]{1,0:T(8,128)(2,1)S(1)}, bf16[384,512]{1,0:T(8,128)(2,1)}, u32[]{:S(2)}) copy-start(bf16[384,512]{1,0:T(8,128)(2,1)} %get-tuple-element.5) | copy-start | bytes 1179652
